TPU v7x, 32 devices: a whole 2x2x4 slice. The times are simulated.
32 devices in a mesh: fsdp: 16 (over z, y, core), grp: 2 (over x).
Axes of the slice: x: 2, y: 2, z: 4, core: 2. Of those that a mesh axis runs over, the one named last changes fastest.
Arguments:
- hidden: bfloat16 [8192, 3072], P('fsdp', 'grp'), may hold values from -16 to 16
- queries: bfloat16 [8192, 1536], P('fsdp', 'grp'), may hold values from -6 to 6
- attn_keys: bfloat16 [8192, 1536], P('fsdp', 'grp'), may hold values from -6 to 6
- w_value: bfloat16 [1536, 3072], P('fsdp', 'grp'), may hold values from -1 to 1
- w_out: bfloat16 [1536, 3072], P('fsdp', 'grp'), may hold values from -1 to 1
- alpha: float32 [3072], P('grp'), may hold values from 0.05 to 0.5
- out_grad: bfloat16 [8192, 3072], P('fsdp', 'grp'), may hold values from -6 to 6
Outputs:
- new_hidden: bfloat16 [8192, 3072], P('fsdp', 'grp')
- grad_hidden: bfloat16 [8192, 3072], P('fsdp', 'grp')
- grad_queries: bfloat16 [8192, 1536], P('fsdp', 'grp')
- grad_keys: bfloat16 [8192, 1536], P('fsdp', 'grp')
- grad_w_value: float32 [1536, 3072], P('fsdp', 'grp')
- grad_w_out: float32 [1536, 3072], P('fsdp', 'grp')
All inputs are finite; a program needn't handle non-finite values.
Results may differ from a plain program's by a relative error of at most 0.012.
The roundings to bfloat16 on the way count: a program that leaves them out, or rounds other values in their place, can miss the bound.
Values may be sent and summed in bfloat16 or wider, within the bound.
A program may use at most 192 MiB of HBM per device.

v0:
```python
import jax
import jax.numpy as jnp
from jax import lax
from jax.sharding import PartitionSpec as P

D = 3072
HS = 128
EPS = 1e-06


def contract_last(left, right):
    return lax.dot_general(
        left, right, (((1,), (1,)), ((), ())), preferred_element_type=jnp.float32
    )


def contract_first(left, right):
    return lax.dot_general(
        left, right, (((0,), (0,)), ((), ())), preferred_element_type=jnp.float32
    )


def causal_probs(query_head, key_head):
    length = query_head.shape[0]
    score_scale = query_head.shape[1] ** (-0.5)
    scores = contract_last(query_head, key_head) * score_scale
    row_pos = lax.broadcasted_iota(jnp.int32, (length, length), 0)
    col_pos = lax.broadcasted_iota(jnp.int32, (length, length), 1)
    scores = jnp.where(row_pos >= col_pos, scores, -1e30)
    row_peak = jnp.max(scores, axis=1, keepdims=True)
    exp_terms = jnp.exp(scores - row_peak)
    return exp_terms / jnp.sum(exp_terms, axis=1, keepdims=True)


def head_forward(items):
    query_head, key_head, value_head = items
    attn_prob = causal_probs(query_head, key_head)
    return jnp.dot(
        attn_prob.astype(jnp.bfloat16), value_head, preferred_element_type=jnp.float32
    ).astype(jnp.bfloat16)


def head_backward(items):
    query_head, key_head, value_head, grad_head = items
    score_scale = query_head.shape[1] ** (-0.5)
    attn_prob = causal_probs(query_head, key_head)
    prob_half = attn_prob.astype(jnp.bfloat16)
    grad_prob = contract_last(grad_head, value_head)
    row_delta = jnp.sum(attn_prob * grad_prob, axis=1, keepdims=True)
    grad_score = (attn_prob * (grad_prob - row_delta)).astype(jnp.bfloat16)
    grad_query = (
        jnp.dot(grad_score, key_head, preferred_element_type=jnp.float32) * score_scale
    ).astype(jnp.bfloat16)
    grad_key = (contract_first(grad_score, query_head) * score_scale).astype(jnp.bfloat16)
    grad_value = contract_first(prob_half, grad_head).astype(jnp.bfloat16)
    return (grad_query, grad_key, grad_value)


def split_heads(block):
    return block.reshape(block.shape[0], -1, HS).transpose(1, 0, 2)


def join_heads(stacked):
    return stacked.transpose(1, 0, 2).reshape(stacked.shape[1], -1)


def shards(hidden, queries, attn_keys, w_value, w_out, alpha, out_grad):
    half_width = hidden.shape[1]
    value_rows = w_value.astype(jnp.float32)
    out_rows = w_out.astype(jnp.float32)
    row_sums = lax.psum(
        (jnp.sum(value_rows * value_rows, axis=1), jnp.sum(out_rows * out_rows, axis=1)), "grp"
    )
    norm_v = jnp.sqrt(row_sums[0] + EPS)[:, None]
    norm_o = jnp.sqrt(row_sums[1] + EPS)[:, None]
    unit_v = value_rows / norm_v
    unit_o = out_rows / norm_o
    weight_v, weight_o = (
        lax.all_gather(unit_v.astype(jnp.bfloat16), "fsdp", axis=0, tiled=True),
        lax.all_gather(unit_o.astype(jnp.bfloat16), "fsdp", axis=0, tiled=True),
    )
    value_parts = contract_last(hidden, weight_v)
    values_mine = lax.psum_scatter(value_parts, "grp", scatter_dimension=1, tiled=True).astype(
        jnp.bfloat16
    )
    q_heads = split_heads(queries)
    k_heads = split_heads(attn_keys)
    v_heads = split_heads(values_mine)
    attn_mine = join_heads(lax.map(head_forward, (q_heads, k_heads, v_heads)))
    attn_all = lax.all_gather(attn_mine, "grp", axis=1, tiled=True)
    proj = jnp.dot(attn_all, weight_o, preferred_element_type=jnp.float32)
    hidden_f = hidden.astype(jnp.float32)
    keep_rate = 1.0 - alpha
    moments = lax.psum(
        (
            jnp.sum(proj * proj, axis=1),
            jnp.sum(keep_rate * keep_rate * hidden_f * hidden_f, axis=1),
            jnp.sum(keep_rate * alpha * hidden_f * proj, axis=1),
            jnp.sum(alpha * alpha * proj * proj, axis=1),
        ),
        "grp",
    )
    proj_rs = lax.rsqrt(moments[0] / D + EPS)[:, None]
    cross_sum = moments[2][:, None]
    alpha_sum = moments[3][:, None]
    mix_mean = (moments[1][:, None] + 2.0 * proj_rs * cross_sum + proj_rs * proj_rs * alpha_sum) / D
    mix_rs = lax.rsqrt(mix_mean + EPS)
    mixed = hidden_f + alpha * (proj * proj_rs - hidden_f)
    new_hidden = (mixed * mix_rs).astype(jnp.bfloat16)
    grad_out = out_grad.astype(jnp.float32)
    grad_sums = lax.psum(
        (
            jnp.sum(grad_out * keep_rate * hidden_f, axis=1),
            jnp.sum(grad_out * alpha * proj, axis=1),
        ),
        "grp",
    )
    grad_mean = (grad_sums[0][:, None] + proj_rs * grad_sums[1][:, None]) / D
    grad_mix = mix_rs * (grad_out - mixed * mix_rs * mix_rs * grad_mean)
    grad_pn = grad_mix * alpha
    proj_mean = (
        mix_rs * grad_sums[1][:, None]
        - mix_rs * mix_rs * mix_rs * grad_mean * (cross_sum + proj_rs * alpha_sum)
    ) / D
    grad_res = grad_mix * keep_rate
    grad_proj = proj_rs * (grad_pn - proj * proj_rs * proj_rs * proj_mean)
    grad_proj_b = grad_proj.astype(jnp.bfloat16)
    grad_attn_parts = contract_last(grad_proj_b, weight_o)
    grad_attn = lax.psum_scatter(grad_attn_parts, "grp", scatter_dimension=1, tiled=True).astype(
        jnp.bfloat16
    )
    grad_q, grad_k, grad_v = lax.map(
        head_backward, (q_heads, k_heads, v_heads, split_heads(grad_attn))
    )
    grad_values = lax.all_gather(join_heads(grad_v), "grp", axis=1, tiled=True)
    grad_hidden = (
        grad_res + jnp.dot(grad_values, weight_v, preferred_element_type=jnp.float32)
    ).astype(jnp.bfloat16)
    owned = lax.psum_scatter(
        jnp.concatenate(
            (contract_first(grad_values, hidden), contract_first(attn_all, grad_proj_b)), axis=1
        ),
        "fsdp",
        scatter_dimension=0,
        tiled=True,
    )
    gw_v_own = owned[:, :half_width]
    gw_o_own = owned[:, half_width:]
    row_dot = lax.psum(
        (jnp.sum(gw_v_own * unit_v, axis=1), jnp.sum(gw_o_own * unit_o, axis=1)), "grp"
    )
    grad_w_value = (gw_v_own - unit_v * row_dot[0][:, None]) / norm_v
    grad_w_out = (gw_o_own - unit_o * row_dot[1][:, None]) / norm_o
    return (
        new_hidden,
        grad_hidden,
        join_heads(grad_q),
        join_heads(grad_k),
        grad_w_value,
        grad_w_out,
    )


def solution(mesh):
    placed = (
        P("fsdp", "grp"),
        P("fsdp", "grp"),
        P("fsdp", "grp"),
        P("fsdp", "grp"),
        P("fsdp", "grp"),
        P("grp"),
        P("fsdp", "grp"),
    )
    return jax.shard_map(
        shards,
        mesh=mesh,
        in_specs=placed,
        out_specs=(
            P("fsdp", "grp"),
            P("fsdp", "grp"),
            P("fsdp", "grp"),
            P("fsdp", "grp"),
            P("fsdp", "grp"),
            P("fsdp", "grp"),
        ),
        check_vma=False,
    )
```

profile of v0, /device:TPU:0, one launch (start us, length us, event | category | flops | bytes accessed | tf_op | source)
XLA Modules:
  0.0 593.8 jit_solution(14473532207321060292)
XLA Ops:
  8.5 5.9 all-reduce.2
  14.4 1.8 fusion.60
  16.2 55.0 %all-gather.5.cloned.1.call-done = bf16[1536,1536]{1,0:T(8,128)(2,1)} async-done(((bf16[96,1536]{1,0:T(8,128)(2,1)}), bf16[1536,1536]{1,0:T(8,128)(2,1)}) %all-gather.5.cloned.1.call-update) | async-done | bytes 4718608 | tf_op jit(solution)/shard_map/all_gather | solution.py:79
  71.3 7.1 %convolution_bitcast_fusion = f32[512,1536]{0,1:T(8,128)} fusion(bf16[1536,1536]{1,0:T(8,128)(2,1)} %all-gather.5.cloned.1.call-done, bf16[512,1536]{1,0:T(8,128)(2,1)} %param.11), kind=kOutput, calls=%fused_computation.68 | convolution fusion | flops 2415919104 | bytes 9437184 | tf_op jit(solution)/shard_map/dot_general | solution.py:12
  81.6 39.0 %reduce-scatter.6.cloned.1.call-done = f32[512,768]{0,1:T(8,128)} async-done(((f32[512,1536]{0,1:T(8,128)}), f32[512,768]{0,1:T(8,128)}) %reduce-scatter.6.cloned.1.call-update) | async-done | bytes 1572880 | tf_op jit(solution)/shard_map/reduce_scatter | solution.py:83
  123.3 11.8 %while.24 = (s32[]{:T(128)}, bf16[6,512,128]{1,2,0:T(8,128)(2,1)S(1)}, bf16[6,512,128]{2,1,0:T(8,128)(2,1)S(1)}, bf16[6,512,128]{2,1,0:T(8,128)(2,1)S(1)}, bf16[6,512,128]{2,1,0:T(8,128)(2,1)}, /*index=5*/s32[]{:T(128)}) while((s32[]{:T(128)}, bf16[6,512,128]{1,2,0:T(8,128)(2,1)S(1)}, bf16[6,512,128]{2,1,0:T(8,128)(2,1)S(1)}, ...), condition=%wide.region_6.7_spmd, body=%wide.region_3.6_spmd.sunk | while | flops 136641536 | bytes 4205653 | solution.py:89
  136.1 40.5 %all-gather.9.cloned.1.call-done = bf16[1536,1536]{1,0:T(8,128)(2,1)} async-done(((bf16[96,1536]{1,0:T(8,128)(2,1)}), bf16[1536,1536]{1,0:T(8,128)(2,1)}) %all-gather.9.cloned.1.call-update) | async-done | bytes 4718608 | tf_op jit(solution)/shard_map/all_gather | solution.py:80
  176.6 27.7 %all-gather.7.cloned.1.call-done = bf16[512,1536]{0,1:T(8,128)(2,1)} async-done(((bf16[512,768]{0,1:T(8,128)(2,1)}), bf16[512,1536]{0,1:T(8,128)(2,1)}) %all-gather.7.cloned.1.call-update) | async-done | bytes 1572880 | tf_op jit(solution)/shard_map/all_gather | solution.py:90
  204.3 8.4 %fusion.43 = (f32[512]{0:T(512)S(1)}, f32[512]{0:T(512)S(1)}, f32[512]{0:T(512)S(1)}, f32[512]{0:T(512)S(1)}, f32[512]{0:T(512)S(1)}, /*index=5*/f32[512]{0:T(512)S(1)}, f32[512,1536]{1,0:T(8,128)S(1)}) fusion(bf16[512,1536]{1,0:T(8,128)(2,1)} %param.17, f32[1536]{0:T(1024)S(1)} %copy-done.14, f32[1536]{0:T(1024)S(1)} %get-tuple-element.182, ...), kind=kOutput, calls=%fused_computation.72 | convolution fusion | flops 2430858240 | bytes 12625920 | tf_op jit(solution)/shard_map/dot_general | solution.py:91
  212.7 6.9 %all-reduce.1 = (f32[512]{0:T(512)S(1)}, f32[512]{0:T(512)S(1)}, f32[512]{0:T(512)S(1)}, f32[512]{0:T(512)S(1)}, f32[512]{0:T(512)S(1)}, /*index=5*/f32[512]{0:T(512)S(1)}) all-reduce(f32[512]{0:T(512)S(1)} %get-tuple-element.126, f32[512]{0:T(512)S(1)} %get-tuple-element.130, ...), channel_id=1, replica_groups=mesh['fsdp'=16,'grp'=2] {'grp'}, use_global_device_ids=true, to_apply=%region_16.17 | all-reduce | flops 3072 | bytes 24576 | tf_op jit(solution)/shard_map/psum | solution.py:94
  219.7 4.5 multiply_convert_fusion.1
  225.4 4.3 fusion.65
  229.7 44.7 %reduce-scatter.8.cloned.1.call-done = f32[512,768]{1,0:T(8,128)} async-done(((f32[512,1536]{1,0:T(8,128)}), f32[512,768]{1,0:T(8,128)}) %reduce-scatter.8.cloned.1.call-update) | async-done | bytes 1572880 | tf_op jit(solution)/shard_map/reduce_scatter | solution.py:129
  278.2 47.0 %while.25 = (s32[]{:T(128)}, bf16[6,512,128]{1,2,0:T(8,128)(2,1)}, bf16[6,512,128]{1,2,0:T(8,128)(2,1)S(1)}, bf16[6,512,128]{1,2,0:T(8,128)(2,1)S(1)}, bf16[6,51...) while((s32[]{:T(128)}, bf16[6,512,128]{1,2,0:T(8,128)(2,1)}, ...), condition=%wide.region_26.27_spmd, body=%wide.region_22.26_spmd.sunk | while | flops 340589056 | bytes 11821177 | solution.py:132
  326.2 8.5 %fusion.67 = f32[1536,1536]{0,1:T(8,128)} fusion(bf16[512,1536]{0,1:T(8,128)(2,1)} %all-gather.7.cloned.1.call-done, bf16[512,1536]{1,0:T(8,128)(2,1)} %copy-done.11), kind=kOutput, calls=%fused_computation.114 | convolution fusion | flops 2415919104 | bytes 12582912 | tf_op jit(solution)/shard_map/dot_general | solution.py:18
  334.7 18.8 %all-gather.11.cloned.1.call-done = bf16[512,1536]{0,1:T(8,128)(2,1)} async-done(((bf16[512,768]{0,1:T(8,128)(2,1)}), bf16[512,1536]{0,1:T(8,128)(2,1)}) %all-gather.11.cloned.1.call-update) | async-done | bytes 1572880 | tf_op jit(solution)/shard_map/all_gather | solution.py:135
  353.5 4.2 fusion.66
  357.8 7.2 %pad_maximum_fusion = f32[1536,3072]{0,1:T(8,128)} fusion(f32[1536,1536]{0,1:T(8,128)S(1)} %copy-done, f32[1536,1536]{0,1:T(8,128)S(1)} %fusion.66), kind=kLoop, calls=%fused_computation.57 | loop fusion | flops 4718592 | bytes 37748736 | tf_op jit(solution)/shard_map/concatenate | solution.py:140
  365.0 18.7 %copy.57 = f32[1536,3072]{1,0:T(8,128)} copy(f32[1536,3072]{0,1:T(8,128)} %pad_maximum_fusion) | data formatting | bytes 37748736
  387.1 9.9 %fusion.51 = bf16[512,1536]{1,0:T(8,128)(2,1)} fusion(bf16[512,1536]{0,1:T(8,128)(2,1)} %all-gather.11.cloned.1.call-done, bf16[1536,1536]{1,0:T(8,128)(2,1)} %all-gather.5.cloned.1.call-done, bf16[512,1536]{1,0:T(8,128)(2,1)S(1)} %copy-done.9, f32[512]{0:T(512)S(1)} %get-tuple-element.187, f32[1536]{0:T(1024)S(1)} %get-tuple-element.185, ...), kind=kOutput, calls=%fused_computation.82 | convolution fusion | flops 2426929152 | bytes 14174208 | tf_op jit(solution)/shard_map/dot_general | solution.py:137
  397.0 180.8 %reduce-scatter.10.cloned.1.call-done = f32[96,3072]{1,0:T(8,128)} async-done(((f32[1536,3072]{1,0:T(8,128)}), f32[96,3072]{1,0:T(8,128)}) %reduce-scatter.10.cloned.1.call-update) | async-done | bytes 1179664 | tf_op jit(solution)/shard_map/reduce_scatter | solution.py:139
  577.9 1.6 multiply_reduce_fusion.2
  579.5 4.9 all-reduce
  584.4 2.5 subtract_divide_fusion
  (168 shorter events, 75.7 us)
Async XLA Ops:
  7.2 64.1 %all-gather.5.cloned.1.call-start = ((), (), s32[]{:S(2)}) async-start(), calls=%async_computation.3 | async-start | bytes 5013504 | tf_op jit(solution)/shard_map/all_gather | solution.py:79
  16.2 104.4 %reduce-scatter.6.cloned.1.call-start = ((), (), s32[]{:S(2)}) async-start(), calls=%async_computation.4 | async-start | bytes 4718592 | tf_op jit(solution)/shard_map/reduce_scatter | solution.py:83
  78.4 1.0 copy-start.2
  78.4 1.9 copy-start.12
  78.4 2.5 copy-start.13
  78.4 98.1 %all-gather.9.cloned.1.call-start = ((), (), s32[]{:S(2)}) async-start(), calls=%async_computation.6 | async-start | bytes 5013504 | tf_op jit(solution)/shard_map/all_gather | solution.py:80
  80.2 124.1 %all-gather.7.cloned.1.call-start = ((), (), s32[]{:S(2)}) async-start(), calls=%async_computation.5 | async-start | bytes 2359296 | tf_op jit(solution)/shard_map/all_gather | solution.py:90
  123.3 12.8 %copy-start.14 = (f32[1536]{0:T(1024)S(1)}, f32[1536]{0:T(1024)}, u32[]{:S(2)}) copy-start(f32[1536]{0:T(1024)} %param.16) | copy-start | bytes 18436
  135.1 0.9 copy-start.5
  135.1 69.2 %copy-start.7 = (bf16[6,512,128]{2,1,0:T(8,128)(2,1)}, bf16[6,512,128]{2,1,0:T(8,128)(2,1)S(1)}, u32[]{:S(2)}) copy-start(bf16[6,512,128]{2,1,0:T(8,128)(2,1)S(1)} %get-tuple-element.351) | copy-start | bytes 2359300
  135.1 69.2 %copy-start.8 = (bf16[6,512,128]{2,1,0:T(8,128)(2,1)}, bf16[6,512,128]{2,1,0:T(8,128)(2,1)S(1)}, u32[]{:S(2)}) copy-start(bf16[6,512,128]{2,1,0:T(8,128)(2,1)S(1)} %get-tuple-element.352) | copy-start | bytes 2359300
  136.0 138.4 %reduce-scatter.8.cloned.1.call-start = ((), (), s32[]{:S(2)}) async-start(), calls=%async_computation.7 | async-start | bytes 4718592 | tf_op jit(solution)/shard_map/reduce_scatter | solution.py:129
  212.7 11.5 %copy-start.6 = (f32[512,1536]{1,0:T(8,128)}, f32[512,1536]{1,0:T(8,128)S(1)}, u32[]{:S(2)}) copy-start(f32[512,1536]{1,0:T(8,128)S(1)} %get-tuple-element.189) | copy-start | bytes 9437188
  219.7 5.7 copy-start.15
  224.2 1.1 copy-start.11
  229.7 123.8 %all-gather.11.cloned.1.call-start = ((), (), s32[]{:S(2)}) async-start(), calls=%async_computation.8 | async-start | bytes 2359296 | tf_op jit(solution)/shard_map/all_gather | solution.py:135
  325.3 0.9 copy-start.3
  326.2 27.4 %copy-start.10 = (bf16[512,1536]{1,0:T(8,128)(2,1)S(1)}, bf16[512,1536]{1,0:T(8,128)(2,1)}, u32[]{:S(2)}) copy-start(bf16[512,1536]{1,0:T(8,128)(2,1)} %param.11) | copy-start | bytes 4718596
  326.2 251.7 %reduce-scatter.10.cloned.1.call-start = ((), (), s32[]{:S(2)}) async-start(), calls=%async_computation.9 | async-start | bytes 20054016 | tf_op jit(solution)/shard_map/reduce_scatter | solution.py:139
  353.5 4.3 copy-start
  383.6 1.1 copy-start.4
  383.7 3.4 copy-start.9
  387.1 190.8 %copy-start.1 = (bf16[96,1536]{1,0:T(8,128)(2,1)S(1)}, bf16[96,1536]{1,0:T(8,128)(2,1)}, u32[]{:S(2)}) copy-start(bf16[96,1536]{1,0:T(8,128)(2,1)} %param.14) | copy-start | bytes 884740
Sparse Core Ops, SparseCore 0:
  16.3 54.9 all-gather.4
  78.6 41.9 reduce-scatter.5
  123.4 53.1 all-gather.8
  178.6 25.7 all-gather.6
  229.8 44.5 reduce-scatter.7
  326.3 27.1 all-gather.10
  383.8 194.0 reduce-scatter.9
where the time goes:
time: 595 us; the launch traced here: 594 us
  waiting for transfers between devices  407 us (68%)
  matrix products  89.7 us (15%)
  local copies, waits for them, and re-layouts  37.6 us (6%)
  other arithmetic  26.8 us (5%)
  blocking collectives  17.7 us (3%)
  between operations  14.3 us (2%)
    reduce_scatter x1, waiting for transfers between devices, shards(): lax.psum_scatter(jnp.concatenate((contract_first(grad_values, hidden), co...  181 us
    all_gather x1, waiting for transfers between devices, shards(): lax.all_gather(unit_v.astype(jnp.bfloat16), 'fsdp', axis=0, tiled=True)  55 us
    reduce_scatter x1, waiting for transfers between devices, shards(): lax.psum_scatter(grad_attn_parts, 'grp', scatter_dimension=1, tiled=True)  44.7 us
    all_gather x1, waiting for transfers between devices, shards(): lax.all_gather(unit_o.astype(jnp.bfloat16), 'fsdp', axis=0, tiled=True)  40.5 us
    reduce_scatter x1, waiting for transfers between devices, shards(): lax.psum_scatter(value_parts, 'grp', scatter_dimension=1, tiled=True)  39 us
    dot_general x20, matrix products, contract_last(): lax.dot_general(left, right, (((1,), (1,)), ((), ())), preferred_element_...  28.7 us
    all_gather x1, waiting for transfers between devices, shards(): attn_all = lax.all_gather(attn_mine, 'grp', axis=1, tiled=True)  27.7 us
    dot_general x14, matrix products, contract_first(): lax.dot_general(left, right, (((0,), (0,)), ((), ())), preferred_element_...  27.4 us
  transfers between devices with their start and end apart: 7, of which 7 were waited for; matrix products, arithmetic and copies ran while one was open for 6% of the time, Pallas kernels for 0%

commit v1 on v0

--- a/solution.py
+++ b/solution.py
@@ -6,6 +6,18 @@
 D = 3072
 HS = 128
 EPS = 1e-06
+
+
+def gather_by_bits(array, axis, dim):
+    ways, here = (lax.axis_size(axis), lax.axis_index(axis))
+    grown, reach = (array, 1)
+    while reach < ways:
+        theirs = lax.ppermute(grown, axis, [(d, d ^ reach) for d in range(ways)])
+        mine_first = jnp.concatenate([grown, theirs], axis=dim)
+        theirs_first = jnp.concatenate([theirs, grown], axis=dim)
+        grown = jnp.where(here & reach == 0, mine_first, theirs_first)
+        reach = 2 * reach
+    return grown
 
 
 def contract_last(left, right):
@@ -76,7 +88,7 @@
     unit_v = value_rows / norm_v
     unit_o = out_rows / norm_o
     weight_v, weight_o = (
-        lax.all_gather(unit_v.astype(jnp.bfloat16), "fsdp", axis=0, tiled=True),
+        gather_by_bits(unit_v.astype(jnp.bfloat16), "fsdp", 0),
         lax.all_gather(unit_o.astype(jnp.bfloat16), "fsdp", axis=0, tiled=True),
     )
     value_parts = contract_last(hidden, weight_v)

time: 595 us -> 654 us (1.099)
  waiting for transfers between devices: 407 us -> 453 us
  starting transfers between devices: 0.29 us -> 6.84 us
    ppermute x0 -> x4, waiting for transfers between devices: none -> 142 us  [gather_by_bits(): theirs = lax.ppermute(grown, axis, [(d, d ^ reach) for d in range(ways)])]
    all_gather x1 -> x0, waiting for transfers between devices: 55 us -> none  [shards(): lax.all_gather(unit_v.astype(jnp.bfloat16), 'fsdp', axis=0, tiled=True)]
    all_gather x1, waiting for transfers between devices: 40.5 us -> 0.03 us  [shards(): lax.all_gather(unit_o.astype(jnp.bfloat16), 'fsdp', axis=0, tiled=True)]
    ppermute x0 -> x4, starting transfers between devices: none -> 6.59 us  [gather_by_bits(): theirs = lax.ppermute(grown, axis, [(d, d ^ reach) for d in range(ways)])]
    unnamed x37 -> x39, local copies, waits for them, and re-layouts: 26.4 us -> 27.8 us
  transfers between devices with their start and end apart: 7 -> 10, of which waited for: 7 -> 9; matrix products, arithmetic and copies ran while one was open for 6% -> 6% of each run, Pallas kernels for 0% -> 0%
where the time goes in v1:
time: 654 us; the launch traced here: 652 us
  waiting for transfers between devices  453 us (69%)
  matrix products  90.6 us (14%)
  local copies, waits for them, and re-layouts  39 us (6%)
  other arithmetic  28.3 us (4%)
  blocking collectives  17.8 us (3%)
  between operations  16 us (2%)
  starting transfers between devices  6.84 us (1%)
    reduce_scatter x1, waiting for transfers between devices, shards(): lax.psum_scatter(jnp.concatenate((contract_first(grad_values, hidden), co...  180 us
    ppermute x4, waiting for transfers between devices, gather_by_bits(): theirs = lax.ppermute(grown, axis, [(d, d ^ reach) for d in range(ways)])  142 us
    reduce_scatter x1, waiting for transfers between devices, shards(): lax.psum_scatter(grad_attn_parts, 'grp', scatter_dimension=1, tiled=True)  44.7 us
    reduce_scatter x1, waiting for transfers between devices, shards(): lax.psum_scatter(value_parts, 'grp', scatter_dimension=1, tiled=True)  41.2 us
    dot_general x20, matrix products, contract_last(): lax.dot_general(left, right, (((1,), (1,)), ((), ())), preferred_element_...  28.7 us
    unnamed x39, local copies, waits for them, and re-layouts  27.8 us
    dot_general x14, matrix products, contract_first(): lax.dot_general(left, right, (((0,), (0,)), ((), ())), preferred_element_...  27.4 us
    all_gather x1, waiting for transfers between devices, shards(): attn_all = lax.all_gather(attn_mine, 'grp', axis=1, tiled=True)  27.1 us
  transfers between devices with their start and end apart: 10, of which 9 were waited for; matrix products, arithmetic and copies ran while one was open for 6% of the time, Pallas kernels for 0%

profile of v1, /device:TPU:0, one launch (start us, length us, event | category | flops | bytes accessed | tf_op | source)
XLA Modules:
  0.0 652.2 jit_solution(8297397027517886657)
XLA Ops:
  9.3 5.9 all-reduce.2
  20.2 13.6 %collective-permute-done.1 = bf16[192,1536]{1,0:T(8,128)(2,1)S(1)} collective-permute-done((bf16[192,1536]{1,0:T(8,128)(2,1)S(1)}, bf16[192,1536]{1,0:T(8,128)(2,1)S(1)}, u32[]{:S(2)}, u32[]{:S(2)}) %collective-permute-start.1) | collective-permute-done | bytes 589856 | tf_op jit(solution)/shard_map/ppermute | solution.py:15
  36.0 25.6 %collective-permute-done.2 = bf16[384,1536]{1,0:T(8,128)(2,1)S(1)} collective-permute-done((bf16[384,1536]{1,0:T(8,128)(2,1)S(1)}, bf16[384,1536]{1,0:T(8,128)(2,1)S(1)}, u32[]{:S(2)}, u32[]{:S(2)}) %collective-permute-start.2) | collective-permute-done | bytes 1179680 | tf_op jit(solution)/shard_map/ppermute | solution.py:15
  63.4 2.5 collective-permute-start.3
  66.0 101.0 %collective-permute-done.3 = bf16[768,1536]{1,0:T(8,128)(2,1)S(1)} collective-permute-done((bf16[768,1536]{1,0:T(8,128)(2,1)}, bf16[768,1536]{1,0:T(8,128)(2,1)S(1)}, u32[]{:S(2)}, u32[]{:S(2)}) %collective-permute-start.3) | collective-permute-done | bytes 2359328 | tf_op jit(solution)/shard_map/ppermute | solution.py:15
  168.3 7.1 %convolution_bitcast_fusion = f32[512,1536]{0,1:T(8,128)} fusion(bf16[512,1536]{1,0:T(8,128)(2,1)} %param.11, bf16[768,1536]{1,0:T(8,128)(2,1)S(1)} %collective-permute-done.3, bf16[768,1536]{1,0:T(8,128)(2,1)} %maximum_select_fusion.1, pred[]{:T(512)S(6)} %eq.12), kind=kOutput, calls=%fused_computation.69 | convolution fusion | flops 2437152768 | bytes 9437185 | tf_op jit(solution)/shard_map/dot_general | solution.py:24
  178.7 41.2 %reduce-scatter.6.cloned.1.call-done = f32[512,768]{0,1:T(8,128)} async-done(((f32[512,1536]{0,1:T(8,128)}), f32[512,768]{0,1:T(8,128)}) %reduce-scatter.6.cloned.1.call-update) | async-done | bytes 1572880 | tf_op jit(solution)/shard_map/reduce_scatter | solution.py:95
  222.6 11.8 %while.24 = (s32[]{:T(128)}, bf16[6,512,128]{1,2,0:T(8,128)(2,1)S(1)}, bf16[6,512,128]{2,1,0:T(8,128)(2,1)S(1)}, bf16[6,512,128]{2,1,0:T(8,128)(2,1)S(1)}, bf16[6,512,128]{2,1,0:T(8,128)(2,1)}, /*index=5*/s32[]{:T(128)}) while((s32[]{:T(128)}, bf16[6,512,128]{1,2,0:T(8,128)(2,1)S(1)}, bf16[6,512,128]{2,1,0:T(8,128)(2,1)S(1)}, ...), condition=%wide.region_6.7_spmd, body=%wide.region_3.6_spmd.sunk | while | flops 136641536 | bytes 4205653 | solution.py:101
  235.4 27.1 %all-gather.4.cloned.1.call-done = bf16[512,1536]{0,1:T(8,128)(2,1)} async-done(((bf16[512,768]{0,1:T(8,128)(2,1)}), bf16[512,1536]{0,1:T(8,128)(2,1)}) %all-gather.4.cloned.1.call-update) | async-done | bytes 1572880 | tf_op jit(solution)/shard_map/all_gather | solution.py:102
  262.5 8.4 %fusion.43 = (f32[512]{0:T(512)S(1)}, f32[512]{0:T(512)S(1)}, f32[512]{0:T(512)S(1)}, f32[512]{0:T(512)S(1)}, f32[512]{0:T(512)S(1)}, /*index=5*/f32[512]{0:T(512)S(1)}, f32[512,1536]{1,0:T(8,128)S(1)}) fusion(bf16[512,1536]{1,0:T(8,128)(2,1)} %param.17, f32[1536]{0:T(1024)S(1)} %copy-done.14, f32[1536]{0:T(1024)S(1)} %get-tuple-element.182, ...), kind=kOutput, calls=%fused_computation.73 | convolution fusion | flops 2430858240 | bytes 12625920 | tf_op jit(solution)/shard_map/dot_general | solution.py:103
  270.9 7.0 %all-reduce.1 = (f32[512]{0:T(512)S(1)}, f32[512]{0:T(512)S(1)}, f32[512]{0:T(512)S(1)}, f32[512]{0:T(512)S(1)}, f32[512]{0:T(512)S(1)}, /*index=5*/f32[512]{0:T(512)S(1)}) all-reduce(f32[512]{0:T(512)S(1)} %get-tuple-element.126, f32[512]{0:T(512)S(1)} %get-tuple-element.130, ...), channel_id=1, replica_groups=mesh['fsdp'=16,'grp'=2] {'grp'}, use_global_device_ids=true, to_apply=%region_16.17 | all-reduce | flops 3072 | bytes 24576 | tf_op jit(solution)/shard_map/psum | solution.py:106
  277.9 4.5 multiply_convert_fusion.1
  283.6 4.3 fusion.67
  288.0 44.7 %reduce-scatter.8.cloned.1.call-done = f32[512,768]{1,0:T(8,128)} async-done(((f32[512,1536]{1,0:T(8,128)}), f32[512,768]{1,0:T(8,128)}) %reduce-scatter.8.cloned.1.call-update) | async-done | bytes 1572880 | tf_op jit(solution)/shard_map/reduce_scatter | solution.py:141
  336.4 47.0 %while.25 = (s32[]{:T(128)}, bf16[6,512,128]{1,2,0:T(8,128)(2,1)}, bf16[6,512,128]{1,2,0:T(8,128)(2,1)S(1)}, bf16[6,512,128]{1,2,0:T(8,128)(2,1)S(1)}, bf16[6,51...) while((s32[]{:T(128)}, bf16[6,512,128]{1,2,0:T(8,128)(2,1)}, ...), condition=%wide.region_26.27_spmd, body=%wide.region_22.26_spmd.sunk | while | flops 340589056 | bytes 11821177 | solution.py:144
  384.4 8.5 %fusion.69 = f32[1536,1536]{0,1:T(8,128)} fusion(bf16[512,1536]{0,1:T(8,128)(2,1)} %all-gather.4.cloned.1.call-done, bf16[512,1536]{1,0:T(8,128)(2,1)} %copy-done.11), kind=kOutput, calls=%fused_computation.120 | convolution fusion | flops 2415919104 | bytes 12582912 | tf_op jit(solution)/shard_map/dot_general | solution.py:30
  392.9 18.6 %all-gather.8.cloned.1.call-done = bf16[512,1536]{0,1:T(8,128)(2,1)} async-done(((bf16[512,768]{0,1:T(8,128)(2,1)}), bf16[512,1536]{0,1:T(8,128)(2,1)}) %all-gather.8.cloned.1.call-update) | async-done | bytes 1572880 | tf_op jit(solution)/shard_map/all_gather | solution.py:147
  411.5 4.2 fusion.68
  415.7 7.2 %pad_maximum_fusion = f32[1536,3072]{0,1:T(8,128)} fusion(f32[1536,1536]{0,1:T(8,128)S(1)} %copy-done, f32[1536,1536]{0,1:T(8,128)S(1)} %fusion.68), kind=kLoop, calls=%fused_computation.57 | loop fusion | flops 4718592 | bytes 37748736 | tf_op jit(solution)/shard_map/concatenate | solution.py:152
  422.9 18.7 %copy.57 = f32[1536,3072]{1,0:T(8,128)} copy(f32[1536,3072]{0,1:T(8,128)} %pad_maximum_fusion) | data formatting | bytes 37748736
  445.0 10.8 %fusion.51 = bf16[512,1536]{1,0:T(8,128)(2,1)} fusion(bf16[512,1536]{0,1:T(8,128)(2,1)} %all-gather.8.cloned.1.call-done, bf16[512,1536]{1,0:T(8,128)(2,1)S(1)} %copy-done.9, f32[512]{0:T(512)S(1)} %get-tuple-element.187, f32[1536]{0:T(1024)S(1)} %get-tuple-element.185, f32[512]{0:T(512)S(1)} %get-tuple-element.184, bf16[768,1536]{1,0:T(8,128)(2,1)} %copy-done.16, ...), kind=kOutput, calls=%fused_computation.83 | convolution fusion | flops 2448162816 | bytes 14174209 | tf_op jit(solution)/shard_map/dot_general | solution.py:149
  455.8 179.8 %reduce-scatter.10.cloned.1.call-done = f32[96,3072]{1,0:T(8,128)} async-done(((f32[1536,3072]{1,0:T(8,128)}), f32[96,3072]{1,0:T(8,128)}) %reduce-scatter.10.cloned.1.call-update) | async-done | bytes 1179664 | tf_op jit(solution)/shard_map/reduce_scatter | solution.py:151
  637.2 4.9 all-reduce
  642.1 2.5 subtract_divide_fusion
  (178 shorter events, 87.6 us)
Async XLA Ops:
  8.0 211.9 %reduce-scatter.6.cloned.1.call-start = ((), (), s32[]{:S(2)}) async-start(), calls=%async_computation.3 | async-start | bytes 4718592 | tf_op jit(solution)/shard_map/reduce_scatter | solution.py:95
  16.3 1.6 collective-permute-start
  18.0 15.8 %collective-permute-start.1 = (bf16[192,1536]{1,0:T(8,128)(2,1)S(1)}, bf16[192,1536]{1,0:T(8,128)(2,1)S(1)}, u32[]{:S(2)}, u32[]{:S(2)}) collective-permute-start(bf16[192,1536]{1,0:T(8,128)(2,1)S(1)} %maximum_select_fusion.5), channel_id=1, source_target_pairs={{0,4},{2,6},{4,0},{6,2},{8,12},{10,14},{12,8},{14,10},{16,20},{18,... | collective-permute-start | bytes 1769480 | tf_op jit(solution)/shard_map/ppermute | solution.py:15
  34.2 27.5 %collective-permute-start.2 = (bf16[384,1536]{1,0:T(8,128)(2,1)S(1)}, bf16[384,1536]{1,0:T(8,128)(2,1)S(1)}, u32[]{:S(2)}, u32[]{:S(2)}) collective-permute-start(bf16[384,1536]{1,0:T(8,128)(2,1)S(1)} %maximum_select_fusion.2), channel_id=1, source_target_pairs={{0,8},{2,10},{4,12},{6,14},{8,0},{10,2},{12,4},{14,6},{16,24},{18,... | collective-permute-start | bytes 3538952 | tf_op jit(solution)/shard_map/ppermute | solution.py:15
  63.4 103.5 %collective-permute-start.3 = (bf16[768,1536]{1,0:T(8,128)(2,1)}, bf16[768,1536]{1,0:T(8,128)(2,1)S(1)}, u32[]{:S(2)}, u32[]{:S(2)}) collective-permute-start(bf16[768,1536]{1,0:T(8,128)(2,1)} %maximum_select_fusion.1), channel_id=1, source_target_pairs={{0,16},{2,18},{4,20},{6,22},{8,24},{10,26},{12,28},{14,30},{16,0},... | collective-permute-start | bytes 7077896 | tf_op jit(solution)/shard_map/ppermute | solution.py:15
  167.0 1.4 copy-start.16
  175.5 1.9 copy-start.12
  175.5 2.5 copy-start.13
  175.5 59.9 %all-gather.6.cloned.1.call-start = ((), (), s32[]{:S(2)}) async-start(), calls=%async_computation.5 | async-start | bytes 5013504 | tf_op jit(solution)/shard_map/all_gather | solution.py:92
  177.3 85.2 %all-gather.4.cloned.1.call-start = ((), (), s32[]{:S(2)}) async-start(), calls=%async_computation.4 | async-start | bytes 2359296 | tf_op jit(solution)/shard_map/all_gather | solution.py:102
  222.6 12.8 %copy-start.14 = (f32[1536]{0:T(1024)S(1)}, f32[1536]{0:T(1024)}, u32[]{:S(2)}) copy-start(f32[1536]{0:T(1024)} %param.16) | copy-start | bytes 18436
  234.4 28.1 %copy-start.7 = (bf16[6,512,128]{2,1,0:T(8,128)(2,1)}, bf16[6,512,128]{2,1,0:T(8,128)(2,1)S(1)}, u32[]{:S(2)}) copy-start(bf16[6,512,128]{2,1,0:T(8,128)(2,1)S(1)} %get-tuple-element.351) | copy-start | bytes 2359300
  234.4 28.1 %copy-start.8 = (bf16[6,512,128]{2,1,0:T(8,128)(2,1)}, bf16[6,512,128]{2,1,0:T(8,128)(2,1)S(1)}, u32[]{:S(2)}) copy-start(bf16[6,512,128]{2,1,0:T(8,128)(2,1)S(1)} %get-tuple-element.352) | copy-start | bytes 2359300
  235.3 97.3 %reduce-scatter.8.cloned.1.call-start = ((), (), s32[]{:S(2)}) async-start(), calls=%async_computation.6 | async-start | bytes 4718592 | tf_op jit(solution)/shard_map/reduce_scatter | solution.py:141
  270.9 11.5 %copy-start.6 = (f32[512,1536]{1,0:T(8,128)}, f32[512,1536]{1,0:T(8,128)S(1)}, u32[]{:S(2)}) copy-start(f32[512,1536]{1,0:T(8,128)S(1)} %get-tuple-element.189) | copy-start | bytes 9437188
  277.9 5.7 copy-start.15
  282.4 1.1 copy-start.11
  287.9 123.6 %all-gather.8.cloned.1.call-start = ((), (), s32[]{:S(2)}) async-start(), calls=%async_computation.7 | async-start | bytes 2359296 | tf_op jit(solution)/shard_map/all_gather | solution.py:147
  384.3 27.2 %copy-start.10 = (bf16[512,1536]{1,0:T(8,128)(2,1)S(1)}, bf16[512,1536]{1,0:T(8,128)(2,1)}, u32[]{:S(2)}) copy-start(bf16[512,1536]{1,0:T(8,128)(2,1)} %param.11) | copy-start | bytes 4718596
  384.3 251.3 %reduce-scatter.10.cloned.1.call-start = ((), (), s32[]{:S(2)}) async-start(), calls=%async_computation.8 | async-start | bytes 20054016 | tf_op jit(solution)/shard_map/reduce_scatter | solution.py:151
  411.5 4.3 copy-start
  441.6 1.1 copy-start.4
  441.6 3.4 copy-start.9
  445.0 190.6 %copy-start.1 = (bf16[96,1536]{1,0:T(8,128)(2,1)S(1)}, bf16[96,1536]{1,0:T(8,128)(2,1)}, u32[]{:S(2)}) copy-start(bf16[96,1536]{1,0:T(8,128)(2,1)} %param.14) | copy-start | bytes 884740
  (3 other events, 2.7 us)
Sparse Core Ops, SparseCore 0:
  175.6 44.2 reduce-scatter.5
  288.0 44.5 reduce-scatter.7
Sparse Core Ops, SparseCore 1:
  178.9 53.8 all-gather.5
  235.4 27.0 all-gather.3
  384.4 27.0 all-gather.7
  441.7 193.8 reduce-scatter.9
